TPU v7x, 32 devices: a whole 2x2x4 slice. The times are simulated.
32 devices in a mesh: seq: 8 (over z, y), tensor: 4 (over x, core).
Axes of the slice: x: 2, y: 2, z: 4, core: 2. Of those that a mesh axis runs over, the one named last changes fastest.
Arguments:
- queries: bfloat16 [2048, 8192], P('seq', 'tensor'), may hold values from -4 to 4, as said below
- keys: bfloat16 [2048, 1024], P('seq', 'tensor'), may hold values from -96 to 96, as said below
- values: bfloat16 [2048, 1024], P('seq', 'tensor'), may hold values from -6 to 6
- block_pos: int32 [16], replicated, may hold values from 0 to 15, each once
Outputs:
- attended: bfloat16 [2048, 8192], P('seq')
Inputs may be any that keep to these rules, and one draw needn't show every extreme that they name: block_pos is a permutation of 0 to 15. real-valued queries. real-valued keys.
All inputs are finite; a program needn't handle non-finite values.
Results may differ from a plain program's by a relative error of at most 0.004.
Values may be sent and summed in bfloat16 or wider, within the bound.
A program may use at most 64 MiB of HBM per device.

v0:
```python
import functools
import math

import jax
import jax.numpy as jnp
from jax import lax
from jax.experimental import pallas as pl
from jax.experimental.pallas import tpu as pltpu
from jax.sharding import PartitionSpec as P

HEAD = 128
GROUP = 8
CUTS = 2
WINDOW = 4
MESH = pl.DeviceIdType.MESH


def kernel(n, T, rows, groups, q_hbm, k_hbm, v_hbm, bp_hbm, out, bp, qv, kv, bias,
           ld_sem, kv_send, kv_recv, x_send, x_recv, c_send, c_recv):
    s = lax.axis_index("seq")
    t = lax.axis_index("tensor")
    heads = groups * GROUP
    hops = T // 2 - 1
    half = rows // 2

    def seq_dev(d):
        return (lax.rem(s + d + n, n), t)

    def x_dev(k):
        return (s, lax.rem(t + 2 * k + T, T))

    sibling = (s, t + 1 - 2 * lax.rem(t, 2))

    loads = []
    for g in range(groups):
        cols = pl.ds(g * HEAD, HEAD)
        pair = []
        for i, src in enumerate((k_hbm, v_hbm)):
            c = pltpu.make_async_copy(src.at[:, cols], kv.at[g, 0, i], ld_sem.at[g, i])
            c.start()
            pair.append(c)
        loads.append(pair)
    q_load = pltpu.make_async_copy(q_hbm, qv, ld_sem.at[groups, 0])
    q_load.start()
    bp_load = pltpu.make_async_copy(bp_hbm, bp, ld_sem.at[groups, 1])
    bp_load.start()

    barrier = pltpu.get_barrier_semaphore()
    peers = [seq_dev(d) for d in (1, 2, -1, -2)] + [sibling]
    peers += [x_dev(k) for k in range(1, hops + 1)]
    for p in peers:
        pl.semaphore_signal(barrier, inc=1, device_id=p, device_id_type=MESH)
    pl.semaphore_wait(barrier, len(peers))

    odd = lax.rem(s, 2)

    cut = rows // CUTS

    def kv_copy(g, i, b, src, d, sent=None):
        part = pl.ds(i % CUTS * cut, cut)
        return pltpu.make_async_remote_copy(
            src_ref=kv.at[g, src, i // CUTS, part], dst_ref=kv.at[g, b, i // CUTS, part],
            send_sem=kv_send.at[g, i, b - 1 if sent is None else sent], recv_sem=kv_recv.at[g, i, b - 1],
            device_id=seq_dev(d), device_id_type=MESH)

    def two(g, i):
        return kv_copy(g, i, 2, 0, 2)

    def three(g, i):
        return kv_copy(g, i, 3, 2, 1)

    def send_own(g):
        for i in range(2 * CUTS):
            if i % CUTS == 0:
                loads[g][i // CUTS].wait()
            two(g, i).start()

            @pl.when(odd == 0)
            def _():
                kv_copy(g, i, 1, 0, 1).start()

    def send_on(g):
        for i in range(2 * CUTS):
            two(g, i).wait_recv()

            @pl.when(odd == 1)
            def _():
                kv_copy(g, i, 1, 2, -1).start()
                three(g, i).start()
                if i % 2:
                    kv_copy(g, i, 1, 0, 1).wait_recv()
                    kv_copy(g, i, 3, 1, 2, 3).start()

            if i % 2 == 0:
                @pl.when(odd == 0)
                def _():
                    three(g, i).start()

    send_own(0)
    bp_load.wait()
    blk = half
    lane = lax.broadcasted_iota(jnp.int32, (blk, blk), 1)
    sub = lax.broadcasted_iota(jnp.int32, (blk, blk), 0)
    for i in range(2):
        qpos = bp[2 * s + i] * blk + sub
        for b in range(WINDOW):
            owner = lax.rem(s - b + n, n)
            for j in range(2):
                kpos = bp[2 * owner + j] * blk + lane
                bias[i * blk:(i + 1) * blk, (2 * b + j) * blk:(2 * b + j + 1) * blk] = (
                    jnp.where(kpos <= qpos, 0.0, -1e30).astype(jnp.float32))
    q_load.wait()
    send_on(0)
    for g in range(1, groups):
        send_own(g)

    def piece(owner, h):
        col = pl.multiple_of((owner * heads + h) * HEAD, HEAD)
        return out.at[:, pl.ds(col, HEAD)]

    def x_copy(k, h, owner):
        return pltpu.make_async_remote_copy(
            src_ref=piece(owner, h), dst_ref=piece(owner, h),
            send_sem=x_send.at[k - 1, h], recv_sem=x_recv.at[k - 1, h],
            device_id=x_dev(k), device_id_type=MESH)

    def c_copy(k, h, owner):
        return pltpu.make_async_remote_copy(
            src_ref=piece(owner, h), dst_ref=piece(owner, h),
            send_sem=c_send.at[k, h], recv_sem=c_recv.at[k, h],
            device_id=sibling, device_id_type=MESH)

    factor = math.log2(math.e) / math.sqrt(HEAD)
    window = WINDOW * rows

    for g in range(groups):
        def arrive(which, g=g):
            for i in range(which * CUTS, (which + 1) * CUTS):
                if i % 2:
                    @pl.when(odd == 0)
                    def _():
                        kv_copy(g, i, 1, 0, 1).wait_recv()
                else:
                    kv_copy(g, i, 1, 0, 1).wait_recv()
                three(g, i).wait_recv()

        arrive(0)

        def one_head(r, _, g=g, late=None):
            h = g * GROUP + r
            qcol = pl.multiple_of(h * HEAD, HEAD)
            ocol = pl.multiple_of((t * heads + h) * HEAD, HEAD)
            keys = kv[g, :, 0].reshape(window, HEAD)
            made = []
            for i in range(2):
                part = slice(i * half, (i + 1) * half)
                q = qv[part, pl.ds(qcol, HEAD)]
                sc = lax.dot_general(q, keys, (((1,), (1,)), ((), ())),
                                     preferred_element_type=jnp.float32)
                sc = sc + bias[part, :]
                top = jnp.max(sc, axis=1, keepdims=True)
                w = jnp.exp2((sc - top) * factor)
                total = jnp.sum(w, axis=1, keepdims=True)
                made.append((part, w.astype(jnp.bfloat16), total))
            if late is not None:
                late(1)
            vals = kv[g, :, 1].reshape(window, HEAD)
            for part, w, total in made:
                mixed = jnp.dot(w, vals, preferred_element_type=jnp.float32)
                out[part, pl.ds(ocol, HEAD)] = (mixed / total).astype(out.dtype)
            for k in range(1, hops + 1):
                x_copy(k, h, t).start()
            c_copy(0, h, t).start()
            return 0

        one_head(0, 0, late=arrive)
        lax.fori_loop(1, GROUP // 2, one_head, 0)
        if g + 1 < groups:
            send_on(g + 1)
        lax.fori_loop(GROUP // 2, GROUP, one_head, 0)

    def forward(h, _):
        for k in range(1, hops + 1):
            owner = lax.rem(t - 2 * k + T, T)
            x_copy(k, h, owner).wait_recv()
            c_copy(k, h, owner).start()
        return 0

    lax.fori_loop(0, heads, forward, 0)

    def finish(h, _):
        for k in range(hops + 1):
            c_copy(k, h, t).wait()
            if k > 0:
                x_copy(k, h, t).wait_send()
        return 0

    lax.fori_loop(0, heads, finish, 0)
    for g in range(groups):
        for i in range(2 * CUTS):
            kv_copy(g, i, 1, 0, 1).wait_send()
            two(g, i).wait_send()
            if i % 2:
                @pl.when(odd == 1)
                def _():
                    three(g, i).wait_send()
                    kv_copy(g, i, 3, 1, 2, 3).wait_send()
            else:
                three(g, i).wait_send()


def body(n, T, queries, keys, values, block_pos):
    rows = queries.shape[0]
    groups = keys.shape[1] // HEAD
    heads = groups * GROUP
    hops = T // 2 - 1
    dma = pltpu.SemaphoreType.DMA
    return pl.pallas_call(
        functools.partial(kernel, n, T, rows, groups),
        out_shape=jax.ShapeDtypeStruct((rows, queries.shape[1] * T), jnp.bfloat16),
        in_specs=[pl.BlockSpec(memory_space=pltpu.HBM)] * 4,
        out_specs=pl.BlockSpec(memory_space=pltpu.VMEM),
        scratch_shapes=[
            pltpu.SMEM(block_pos.shape, jnp.int32),
            pltpu.VMEM((rows, heads * HEAD), jnp.bfloat16),
            pltpu.VMEM((groups, WINDOW, 2, rows, HEAD), jnp.bfloat16),
            pltpu.VMEM((rows, WINDOW * rows), jnp.float32),
            dma((groups + 1, 2)),
            dma((groups, 2 * CUTS, 4)),
            dma((groups, 2 * CUTS, 3)),
            dma((hops, heads)),
            dma((hops, heads)),
            dma((hops + 1, heads)),
            dma((hops + 1, heads)),
        ],
        compiler_params=pltpu.CompilerParams(
            collective_id=0, has_side_effects=True, vmem_limit_bytes=32 * 1024 * 1024),
    )(*(pltpu.with_memory_space_constraint(z, pltpu.HBM)
        for z in (queries, keys, values, block_pos)))


def solution(mesh):
    n, T = mesh.shape["seq"], mesh.shape["tensor"]
    placed = (P("seq", "tensor"), P("seq", "tensor"), P("seq", "tensor"), P())
    return jax.shard_map(functools.partial(body, n, T), mesh=mesh, in_specs=placed,
                         out_specs=P("seq", None), check_vma=False)
```

profile of v0, /device:TPU:0, one launch (start us, length us, event | category | flops | bytes accessed | tf_op | source)
XLA Modules:
  0.0 42.2 jit_solution(10212876147238553132)
XLA Ops:
  0.0 40.2 %shard_map.46 = bf16[256,8192]{1,0:T(8,128)(2,1)S(1)} custom-call(bf16[256,2048]{1,0:T(8,128)(2,1)} %q_hbm.1, bf16[256,256]{1,0:T(8,128)(2,1)} %k_hbm.1, bf16[256,256]{1,0:T(8,128)(2,1)} %v_hbm.1, s32[16]{0:T(128)} %bp_hbm.1), custom_call_target="tpu_custom_call" | custom-call | tf_op jit(solution)/shard_map/pallas_call | solution.py:218
  40.2 2.0 %copy.6 = bf16[256,8192]{1,0:T(8,128)(2,1)} copy(bf16[256,8192]{1,0:T(8,128)(2,1)S(1)} %shard_map.46) | data formatting | bytes 8388608
where the time goes:
time: 42.4 us; the launch traced here: 42.2 us
  Pallas kernels  40.2 us (95%)
  local copies, waits for them, and re-layouts  2.02 us (5%)
    pallas_call x1, Pallas kernels, body(): pl.pallas_call(functools.partial(kernel, n, T, rows, groups), out_shape=j...  40.2 us
    unnamed x1, local copies, waits for them, and re-layouts  2.02 us

commit v1 on v0

v1 whole, which is shorter than its diff:
```python
import functools
import math

import jax
import jax.numpy as jnp
from jax import lax
from jax.experimental import pallas as pl
from jax.experimental.pallas import tpu as pltpu
from jax.sharding import PartitionSpec as P

HEAD = 128
GROUP = 8
CUTS = 2
PIECES = 2 * CUTS
WINDOW = 4
SHARE = 5
CROSS = (0, 1)
BESIDE = (0, 1, 2)
MESH = pl.DeviceIdType.MESH


def kernel(n, T, rows, groups, share, q_hbm, k_hbm, v_hbm, bp_hbm, out, bp, qv, qx, kv, bias,
           ld_sem, kv_send, kv_recv, xk_send, xk_recv, x_send, x_recv, c_send, c_recv):
    s = lax.axis_index("seq")
    t = lax.axis_index("tensor")
    heads = groups * GROUP
    solo = heads - share
    last = groups - 1
    hops = T // 2 - 1
    half = rows // 2
    cut = rows // CUTS

    def seq_dev(d):
        return (lax.rem(s + d + n, n), t)

    def x_dev(k):
        return (s, lax.rem(t + 2 * k + T, T))

    sibling = (s, t + 1 - 2 * lax.rem(t, 2))
    partner = lax.rem(t + 2, T)
    odd = lax.rem(s, 2)

    loads = []
    for g in range(groups):
        cols = pl.ds(g * HEAD, HEAD)
        pair = []
        for i, src in enumerate((k_hbm, v_hbm)):
            c = pltpu.make_async_copy(src.at[:, cols], kv.at[g, 0, i], ld_sem.at[g, i])
            c.start()
            pair.append(c)
        loads.append(pair)
    q_parts = []
    for i, (lo, hi) in enumerate(((solo, heads), (0, solo))):
        if hi > lo:
            cols = pl.ds(lo * HEAD, (hi - lo) * HEAD)
            c = pltpu.make_async_copy(q_hbm.at[:, cols], qv.at[:, cols], ld_sem.at[groups, i])
            c.start()
            q_parts.append(c)
    bp_load = pltpu.make_async_copy(bp_hbm, bp, ld_sem.at[groups + 1, 0])
    bp_load.start()

    barrier = pltpu.get_barrier_semaphore()

    def greet(p):
        pl.semaphore_signal(barrier, inc=1, device_id=p, device_id_type=MESH)

    near = [sibling] + [x_dev(k) for k in range(1, hops + 1)]
    for p in near:
        greet(p)

    @pl.when(odd == 0)
    def _():
        for d in (1, -2, -1):
            greet(seq_dev(d))
        pl.semaphore_wait(barrier, len(near) + 2)

    @pl.when(odd == 1)
    def _():
        for d in (-1, -2):
            greet(seq_dev(d))
        pl.semaphore_wait(barrier, len(near) + 3)

    def kv_copy(g, i, b, src, d, sent):
        part = pl.ds(i % CUTS * cut, cut)
        return pltpu.make_async_remote_copy(
            src_ref=kv.at[g, src, i // CUTS, part], dst_ref=kv.at[g, b, i // CUTS, part],
            send_sem=kv_send.at[g, i, sent], recv_sem=kv_recv.at[g, i, b - 1],
            device_id=seq_dev(d), device_id_type=MESH)

    def got(g, i, b):
        kv_copy(g, i, b, 0, 1, 0).wait_recv()

    def send_own(g, i):
        kv_copy(g, i, 2, 0, 2, 1).start()

        @pl.when(odd == 0)
        def _():
            kv_copy(g, i, 1, 0, 1, 0).start()

    def relay_two(g):
        for i in range(PIECES):
            got(g, i, 2)

            @pl.when(odd == 1)
            def _():
                kv_copy(g, i, 1, 2, -1, 0).start()
                if i in CROSS:
                    kv_copy(g, i, 3, 2, 1, 2).start()

            if i in BESIDE:
                @pl.when(odd == 0)
                def _():
                    kv_copy(g, i, 3, 2, 1, 2).start()

    def relay_one(g):
        for i in range(PIECES):
            got(g, i, 1)
            if i not in BESIDE:
                @pl.when(odd == 1)
                def _():
                    kv_copy(g, i, 3, 1, 2, 3).start()
            if i not in CROSS:
                @pl.when(odd == 0)
                def _():
                    kv_copy(g, i, 3, 1, 2, 3).start()

    def xk_copy(i):
        return pltpu.make_async_remote_copy(
            src_ref=kv.at[last, 0, i], dst_ref=kv.at[groups, 0, i],
            send_sem=xk_send.at[i], recv_sem=xk_recv.at[i],
            device_id=x_dev(1), device_id_type=MESH)

    def xq_copy():
        return pltpu.make_async_remote_copy(
            src_ref=qv.at[:, pl.ds(solo * HEAD, share * HEAD)], dst_ref=qx,
            send_sem=xk_send.at[2], recv_sem=xk_recv.at[2],
            device_id=x_dev(1), device_id_type=MESH)

    for i in range(PIECES):
        if i % CUTS == 0:
            loads[0][i // CUTS].wait()
        send_own(0, i)
    for g in range(1, groups):
        for i in range(PIECES):
            if i % CUTS == 0:
                loads[g][i // CUTS].wait()
                if share and g == last:
                    xk_copy(i // CUTS).start()
            send_own(g, i)
    for c in q_parts:
        c.wait()
        if share and c is q_parts[0]:
            xq_copy().start()

    bp_load.wait()
    blk = half
    lane = lax.broadcasted_iota(jnp.int32, (blk, blk), 1)
    sub = lax.broadcasted_iota(jnp.int32, (blk, blk), 0)
    for i in range(2):
        qpos = bp[2 * s + i] * blk + sub
        for b in range(WINDOW):
            owner = lax.rem(s - b + n, n)
            for j in range(2):
                kpos = bp[2 * owner + j] * blk + lane
                bias[i * blk:(i + 1) * blk, (2 * b + j) * blk:(2 * b + j + 1) * blk] = (
                    jnp.where(kpos <= qpos, 0.0, -1e30).astype(jnp.float32))

    relay_two(0)
    relay_one(0)
    if share:
        for i in range(PIECES):
            if i % CUTS == 0:
                xk_copy(i // CUTS).wait_recv()
            send_own(groups, i)

    def piece(owner, h):
        col = pl.multiple_of((owner * heads + h) * HEAD, HEAD)
        return out.at[:, pl.ds(col, HEAD)]

    def x_copy(k, h, owner):
        return pltpu.make_async_remote_copy(
            src_ref=piece(owner, h), dst_ref=piece(owner, h),
            send_sem=x_send.at[k - 1, h], recv_sem=x_recv.at[k - 1, h],
            device_id=x_dev(k), device_id_type=MESH)

    def c_copy(k, h, owner):
        return pltpu.make_async_remote_copy(
            src_ref=piece(owner, h), dst_ref=piece(owner, h),
            send_sem=c_send.at[k, h], recv_sem=c_recv.at[k, h],
            device_id=sibling, device_id_type=MESH)

    factor = math.log2(math.e) / math.sqrt(HEAD)
    window = WINDOW * rows

    def attend(g, queries, qcol, owner, h):
        qcol = pl.multiple_of(qcol, HEAD)
        ocol = pl.multiple_of((owner * heads + h) * HEAD, HEAD)
        keys = kv[g, :, 0].reshape(window, HEAD)
        made = []
        for i in range(2):
            part = slice(i * half, (i + 1) * half)
            q = queries[part, pl.ds(qcol, HEAD)]
            sc = lax.dot_general(q, keys, (((1,), (1,)), ((), ())),
                                 preferred_element_type=jnp.float32)
            sc = sc + bias[part, :]
            top = jnp.max(sc, axis=1, keepdims=True)
            w = jnp.exp2((sc - top) * factor)
            total = jnp.sum(w, axis=1, keepdims=True)
            made.append((part, w.astype(jnp.bfloat16), total))
        vals = kv[g, :, 1].reshape(window, HEAD)
        for part, w, total in made:
            mixed = jnp.dot(w, vals, preferred_element_type=jnp.float32)
            out[part, pl.ds(ocol, HEAD)] = (mixed / total).astype(out.dtype)

    def own_head(h, _, g):
        attend(g, qv, h * HEAD, t, h)

        @pl.when(h < solo)
        def _():
            for k in range(1, hops + 1):
                x_copy(k, h, t).start()

        c_copy(0, h, t).start()
        return 0

    def partner_head(r, _):
        attend(groups, qx, r * HEAD, partner, solo + r)
        c_copy(1, solo + r, partner).start()
        return 0

    def forward(h, _):
        for k in range(1, hops + 1):
            owner = lax.rem(t - 2 * k + T, T)
            x_copy(k, h, owner).wait_recv()
            c_copy(k, h, owner).start()
        return 0

    total_groups = groups + (1 if share else 0)
    for g in range(groups):
        for i in range(PIECES):
            got(g, i, 3)
        base = g * GROUP
        body = functools.partial(own_head, g=g)
        more = g + 1 < total_groups
        lax.fori_loop(base, base + 2, body, 0)
        if more:
            relay_two(g + 1)
        lax.fori_loop(base + 2, base + 4, body, 0)
        if more:
            relay_one(g + 1)
        lax.fori_loop(base + 4, base + GROUP, body, 0)

    early = solo // 2
    lax.fori_loop(0, early, forward, 0)
    if share:
        for i in range(PIECES):
            got(groups, i, 3)
        xq_copy().wait_recv()
        lax.fori_loop(0, share, partner_head, 0)
    lax.fori_loop(early, solo, forward, 0)

    def finish(h, _):
        for k in range(hops + 1):
            c_copy(k, h, t).wait()

        @pl.when(h < solo)
        def _():
            for k in range(1, hops + 1):
                x_copy(k, h, t).wait_send()

        return 0

    lax.fori_loop(0, heads, finish, 0)
    if share:
        for i in range(2):
            xk_copy(i).wait_send()
        xq_copy().wait_send()
    for g in range(total_groups):
        for i in range(PIECES):
            kv_copy(g, i, 1, 0, 1, 0).wait_send()
            kv_copy(g, i, 2, 0, 2, 1).wait_send()
            for parity, sent, when in ((1, 2, i in CROSS), (0, 2, i in BESIDE),
                                       (1, 3, i not in BESIDE), (0, 3, i not in CROSS)):
                if when:
                    @pl.when(odd == parity)
                    def _():
                        kv_copy(g, i, 3, 0, 1, sent).wait_send()


def body(n, T, queries, keys, values, block_pos):
    rows = queries.shape[0]
    groups = keys.shape[1] // HEAD
    heads = groups * GROUP
    hops = T // 2 - 1
    share = SHARE if hops == 1 and groups > 1 else 0
    total = groups + (1 if share else 0)
    dma = pltpu.SemaphoreType.DMA
    return pl.pallas_call(
        functools.partial(kernel, n, T, rows, groups, share),
        out_shape=jax.ShapeDtypeStruct((rows, queries.shape[1] * T), jnp.bfloat16),
        in_specs=[pl.BlockSpec(memory_space=pltpu.HBM)] * 4,
        out_specs=pl.BlockSpec(memory_space=pltpu.VMEM),
        scratch_shapes=[
            pltpu.SMEM(block_pos.shape, jnp.int32),
            pltpu.VMEM((rows, heads * HEAD), jnp.bfloat16),
            pltpu.VMEM((rows, max(share, 1) * HEAD), jnp.bfloat16),
            pltpu.VMEM((total, WINDOW, 2, rows, HEAD), jnp.bfloat16),
            pltpu.VMEM((rows, WINDOW * rows), jnp.float32),
            dma((groups + 2, 2)),
            dma((total, PIECES, 4)),
            dma((total, PIECES, 3)),
            dma((3,)),
            dma((3,)),
            dma((hops, heads)),
            dma((hops, heads)),
            dma((hops + 1, heads)),
            dma((hops + 1, heads)),
        ],
        compiler_params=pltpu.CompilerParams(
            collective_id=0, has_side_effects=True, vmem_limit_bytes=32 * 1024 * 1024),
    )(*(pltpu.with_memory_space_constraint(z, pltpu.HBM)
        for z in (queries, keys, values, block_pos)))


def solution(mesh):
    n, T = mesh.shape["seq"], mesh.shape["tensor"]
    placed = (P("seq", "tensor"), P("seq", "tensor"), P("seq", "tensor"), P())
    return jax.shard_map(functools.partial(body, n, T), mesh=mesh, in_specs=placed,
                         out_specs=P("seq", None), check_vma=False)
```

time: 42.4 us -> 38.5 us (0.908)
  Pallas kernels: 40.2 us -> 36.4 us
    pallas_call x1, Pallas kernels: 40.2 us -> 36.4 us  [body(): pl.pallas_call(functools.partial(kernel, n, T, rows, groups, share), out_...]
where the time goes in v1:
time: 38.5 us; the launch traced here: 38.4 us
  Pallas kernels  36.4 us (95%)
  local copies, waits for them, and re-layouts  2.02 us (5%)
    pallas_call x1, Pallas kernels, body(): pl.pallas_call(functools.partial(kernel, n, T, rows, groups, share), out_...  36.4 us
    unnamed x1, local copies, waits for them, and re-layouts  2.02 us

profile of v1, /device:TPU:0, one launch (start us, length us, event | category | flops | bytes accessed | tf_op | source)
XLA Modules:
  0.0 38.4 jit_solution(14874193231090065559)
XLA Ops:
  0.0 36.4 %shard_map.46 = bf16[256,8192]{1,0:T(8,128)(2,1)S(1)} custom-call(bf16[256,2048]{1,0:T(8,128)(2,1)} %q_hbm.1, bf16[256,256]{1,0:T(8,128)(2,1)} %k_hbm.1, bf16[256,256]{1,0:T(8,128)(2,1)} %v_hbm.1, s32[16]{0:T(128)} %bp_hbm.1), custom_call_target="tpu_custom_call" | custom-call | tf_op jit(solution)/shard_map/pallas_call | solution.py:298
  36.4 2.0 %copy.6 = bf16[256,8192]{1,0:T(8,128)(2,1)} copy(bf16[256,8192]{1,0:T(8,128)(2,1)S(1)} %shard_map.46) | data formatting | bytes 8388608

commit v2 on v0

v2 whole, which is shorter than its diff:
```python
import functools
import math

import jax
import jax.numpy as jnp
from jax import lax
from jax.experimental import pallas as pl
from jax.experimental.pallas import tpu as pltpu
from jax.sharding import PartitionSpec as P

HEAD = 128
GROUP = 8
CUTS = 2
PIECES = 2 * CUTS
WINDOW = 4
SHARE = (8, 0)
AHEAD = (6, 10)
CROSS = ((0, 1, 2, 3), (0, 1), (0, 1))
BESIDE = ((0, 1, 2, 3), (0, 1, 2, 3), (0, 1, 2, 3))
MESH = pl.DeviceIdType.MESH


def kernel(n, T, rows, groups, share, q_hbm, k_hbm, v_hbm, bp_hbm, out, bp, qv, qx, kv, bias,
           ld_sem, go_sem, own_send, relay_send, two_recv, kind_recv, lend_send, lend_recv,
           x_send, x_recv, c_send, c_recv):
    s = lax.axis_index("seq")
    t = lax.axis_index("tensor")
    core = lax.rem(t, 2)
    heads = groups * GROUP
    keep = tuple(heads - m for m in share)
    last = groups - 1
    every = groups + (1 if any(share) else 0)
    hops = T // 2 - 1
    half = rows // 2
    cut = rows // CUTS

    def cross(g):
        return CROSS[min(g, 2)]

    def beside(g):
        return BESIDE[min(g, 2)]

    def seq_dev(d):
        return (lax.rem(s + d + n, n), t)

    def x_dev(k):
        return (s, lax.rem(t + 2 * k + T, T))

    sibling = (s, t + 1 - 2 * core)
    other = lax.rem(t + 3 - 2 * core, T)
    match = (s, other)
    odd = lax.rem(s, 2)

    def on_core(c):
        return pl.when(core == c)

    def lenders(f):
        for c in range(2):
            if share[c]:
                on_core(c)(functools.partial(f, share[c], keep[c]))

    def borrowers(f):
        for c in range(2):
            if share[c]:
                on_core(1 - c)(functools.partial(f, share[c], keep[c]))

    for g in range(groups):
        cols = pl.ds(g * HEAD, HEAD)
        for i, src in enumerate((k_hbm, v_hbm)):
            pltpu.make_async_copy(src.at[:, cols], kv.at[g, 0, i], ld_sem.at[min(g, 1)]).start()
    q_load = pltpu.make_async_copy(q_hbm, qv, ld_sem.at[2])
    q_load.start()
    bp_load = pltpu.make_async_copy(bp_hbm, bp, ld_sem.at[3])
    bp_load.start()

    barrier = pltpu.get_barrier_semaphore()

    def greet(p):
        pl.semaphore_signal(barrier, inc=1, device_id=p, device_id_type=MESH)

    near = [sibling] + [x_dev(k) for k in range(1, hops + 1)]
    for p in near:
        greet(p)
    borrowers(lambda m, first: greet(match))

    @pl.when(odd == 0)
    def _():
        for d in (1, -2, -1):
            greet(seq_dev(d))

    @pl.when(odd == 1)
    def _():
        for d in (-1, -2):
            greet(seq_dev(d))

    for c in range(2):
        @on_core(c)
        def _():
            pl.semaphore_wait(barrier, len(near) + 2 + (1 if share[c] else 0) + odd)

    def kv_copy(g, i, b, src, d, own=False):
        part = pl.ds(i % CUTS * cut, cut)
        return pltpu.make_async_remote_copy(
            src_ref=kv.at[g, src, i // CUTS, part], dst_ref=kv.at[g, b, i // CUTS, part],
            send_sem=(own_send if own else relay_send).at[g],
            recv_sem=two_recv.at[g, i] if b == 2 else kind_recv.at[g, b // 2, i // CUTS],
            device_id=seq_dev(d), device_id_type=MESH)

    def slots(g, ref, sem):
        return pltpu.make_async_remote_copy(
            src_ref=ref, dst_ref=ref, send_sem=sem, recv_sem=sem,
            device_id=sibling, device_id_type=MESH)

    def got(g, b, kind):
        slots(g, kv.at[g, b, kind], kind_recv.at[g, b // 2, kind]).wait_recv()

    def send_own(g):
        for i in range(PIECES):
            kv_copy(g, i, 2, 0, 2, True).start()

            @pl.when(odd == 0)
            def _():
                kv_copy(g, i, 1, 0, 1, True).start()

    def relay_two(g):
        for i in range(PIECES):
            kv_copy(g, i, 2, 0, 2).wait_recv()

            @pl.when(odd == 1)
            def _():
                kv_copy(g, i, 1, 2, -1).start()
                if i in cross(g):
                    kv_copy(g, i, 3, 2, 1).start()

            if i in beside(g):
                @pl.when(odd == 0)
                def _():
                    kv_copy(g, i, 3, 2, 1).start()

    def relay_one(g, kind):
        got(g, 1, kind)
        for i in range(kind * CUTS, (kind + 1) * CUTS):
            if i not in beside(g):
                @pl.when(odd == 1)
                def _():
                    kv_copy(g, i, 3, 1, 2).start()
            if i not in cross(g):
                @pl.when(odd == 0)
                def _():
                    kv_copy(g, i, 3, 1, 2).start()

    def own_sent(g):
        for parity, count in ((0, 2), (1, 1)):
            @pl.when(odd == parity)
            def _():
                slots(g, kv.at[g, 0:count], own_send.at[g]).wait_send()

    def relays_sent(g):
        ways = len(beside(g)) - len(cross(g))
        for parity, count in ((0, PIECES + ways), (1, 2 * PIECES - ways)):
            @pl.when(odd == parity)
            def _():
                slots(g, kv.at[g, 0:count // 2, 0], relay_send.at[g]).wait_send()

    def keys_lent():
        return pltpu.make_async_remote_copy(
            src_ref=kv.at[last, 0], dst_ref=kv.at[groups, 0],
            send_sem=lend_send.at[0], recv_sem=lend_recv.at[0],
            device_id=match, device_id_type=MESH)

    def queries_lent(m, first):
        return pltpu.make_async_remote_copy(
            src_ref=qv.at[:, pl.ds(first * HEAD, m * HEAD)], dst_ref=qx.at[:, pl.ds(0, m * HEAD)],
            send_sem=lend_send.at[1], recv_sem=lend_recv.at[1],
            device_id=match, device_id_type=MESH)

    def loaded(g):
        pltpu.make_async_copy(kv.at[g, 1], kv.at[g, 0], ld_sem.at[min(g, 1)]).wait()

    loaded(0)

    @on_core(1)
    def _():
        send_own(0)

    if groups > 1:
        ref = kv.at[1:groups, 0]
        pltpu.make_async_copy(ref, ref, ld_sem.at[1]).wait()
    q_load.wait()

    def lend(m, first):
        keys_lent().start()
        queries_lent(m, first).start()

    lenders(lend)

    @on_core(1)
    def _():
        own_sent(0)
        pl.semaphore_signal(go_sem, inc=1, device_id=sibling, device_id_type=MESH)

    @on_core(0)
    def _():
        pl.semaphore_wait(go_sem, 1)
        send_own(0)

    bp_load.wait()
    blk = half
    lane = lax.broadcasted_iota(jnp.int32, (blk, blk), 1)
    sub = lax.broadcasted_iota(jnp.int32, (blk, blk), 0)
    for i in range(2):
        qpos = bp[2 * s + i] * blk + sub
        for b in range(WINDOW):
            owner = lax.rem(s - b + n, n)
            for j in range(2):
                kpos = bp[2 * owner + j] * blk + lane
                bias[i * blk:(i + 1) * blk, (2 * b + j) * blk:(2 * b + j + 1) * blk] = (
                    jnp.where(kpos <= qpos, 0.0, -1e30).astype(jnp.float32))

    relay_two(0)
    for g in range(1, groups):
        send_own(g)

    def pass_on(m, first):
        keys_lent().wait_recv()
        send_own(groups)

    borrowers(pass_on)

    def piece(owner, h, count=1):
        col = pl.multiple_of((owner * heads + h) * HEAD, HEAD)
        return out.at[:, pl.ds(col, count * HEAD)]

    def x_copy(k, h, owner, count=1):
        return pltpu.make_async_remote_copy(
            src_ref=piece(owner, h, count), dst_ref=piece(owner, h, count),
            send_sem=x_send.at[k - 1], recv_sem=x_recv.at[k - 1, h // 2],
            device_id=x_dev(k), device_id_type=MESH)

    def c_copy(k, h, owner, count=1):
        return pltpu.make_async_remote_copy(
            src_ref=piece(owner, h, count), dst_ref=piece(owner, h, count),
            send_sem=c_send.at[k], recv_sem=c_recv.at[k],
            device_id=sibling, device_id_type=MESH)

    factor = math.log2(math.e) / math.sqrt(HEAD)
    window = WINDOW * rows

    def attend(g, jobs, late=None):
        keys = kv[g, :, 0].reshape(window, HEAD)
        made = []
        for queries, qcol, col in jobs:
            qcol = pl.multiple_of(qcol, HEAD)
            col = pl.multiple_of(col, HEAD)
            for i in range(2):
                part = slice(i * half, (i + 1) * half)
                q = queries[part, pl.ds(qcol, HEAD)]
                sc = lax.dot_general(q, keys, (((1,), (1,)), ((), ())),
                                     preferred_element_type=jnp.float32)
                sc = sc + bias[part, :]
                top = jnp.max(sc, axis=1, keepdims=True)
                w = jnp.exp2((sc - top) * factor)
                total = jnp.sum(w, axis=1, keepdims=True)
                made.append((part, col, w.astype(jnp.bfloat16), total))
        if late is not None:
            late()
        vals = kv[g, :, 1].reshape(window, HEAD)
        for part, col, w, total in made:
            mixed = jnp.dot(w, vals, preferred_element_type=jnp.float32)
            out[part, pl.ds(col, HEAD)] = (mixed / total).astype(out.dtype)

    def own_heads(g, first, count, late=None):
        attend(g, [(qv, h * HEAD, (t * heads + h) * HEAD) for h in range(first, first + count)], late)
        for h in range(first, first + count, 2):
            for c in range(2):
                if h < keep[c]:
                    @on_core(c)
                    def _():
                        for k in range(1, hops + 1):
                            x_copy(k, h, t, 2).start()
        c_copy(0, first, t, count).start()

    def lent_heads(r, _, step, first):
        r = r * step
        attend(groups, [(qx, (r + j) * HEAD, (other * heads + first + r + j) * HEAD) for j in range(step)])
        c_copy(hops + 1, first + r, other, step).start()
        return 0

    def forward(h, _):
        h = 2 * h
        for k in range(1, hops + 1):
            owner = lax.rem(t - 2 * k + T, T)
            x_copy(k, h, owner, 2).wait_recv()
            c_copy(k, h, owner, 2).start()
        return 0

    def relay(g, f):
        if g < groups:
            f(g)
        elif g < every:
            borrowers(lambda m, first: f(g))

    def first_relays(g):
        relay_one(g, 0)
        relay_one(g, 1)

    def arrive(g):
        got(g, 3, 0)
        got(g, 3, 1)

    def late():
        relay_one(0, 1)
        got(0, 3, 1)

    for g in range(groups):
        base = g * GROUP
        if g == 0:
            relay_one(0, 0)
            got(0, 3, 0)
            own_heads(0, 0, 2, late)
            own_heads(0, 2, 2)
        else:
            arrive(g)
            own_heads(g, base, 4)
        relay(g + 1, relay_two)
        own_heads(g, base + 4, 4)
        relay(g + 1, first_relays)

    def forwards(first, end):
        lax.fori_loop(first // 2, end // 2, forward, 0)

    done = [0, 0]

    def borrowed(m, first):
        c = 1 - share.index(m)
        stops = [min(x, keep[c]) for x in AHEAD]
        forwards(0, stops[0])
        arrive(groups)
        queries_lent(m, first).wait_recv()
        step = math.gcd(m, 4)
        for r in range(m // step):
            lent_heads(r, 0, step, first)
            if r == 0:
                forwards(stops[0], stops[1])
        done[c] = stops[1]

    borrowers(borrowed)
    for c in range(2):
        @on_core(c)
        def _():
            forwards(done[c], keep[c])

    for g in range(groups):
        relays_sent(g)
        if g > 0:
            own_sent(g)
    on_core(0)(lambda: own_sent(0))

    def settle(m, first):
        relays_sent(groups)
        own_sent(groups)
        c_copy(hops + 1, first, other, m).wait_send()

    borrowers(settle)

    def settle_lent(m, first):
        keys_lent().wait_send()
        queries_lent(m, first).wait_send()
        c_copy(hops + 1, first, t, m).wait_recv()

    lenders(settle_lent)
    c_copy(0, 0, t, heads).wait()

    for c in range(2):
        @on_core(c)
        def _():
            for k in range(1, hops + 1):
                x_copy(k, 0, t, keep[c]).wait_send()
                c_copy(k, 0, t, keep[c]).wait_send()
                c_copy(k, 0, t, keep[1 - c]).wait_recv()


def body(n, T, queries, keys, values, block_pos):
    rows = queries.shape[0]
    groups = keys.shape[1] // HEAD
    heads = groups * GROUP
    hops = T // 2 - 1
    share = SHARE if hops == 1 and groups > 1 else (0, 0)
    every = groups + (1 if any(share) else 0)
    dma = pltpu.SemaphoreType.DMA
    return pl.pallas_call(
        functools.partial(kernel, n, T, rows, groups, share),
        out_shape=jax.ShapeDtypeStruct((rows, queries.shape[1] * T), jnp.bfloat16),
        in_specs=[pl.BlockSpec(memory_space=pltpu.HBM)] * 4,
        out_specs=pl.BlockSpec(memory_space=pltpu.VMEM),
        scratch_shapes=[
            pltpu.SMEM(block_pos.shape, jnp.int32),
            pltpu.VMEM((rows, heads * HEAD), jnp.bfloat16),
            pltpu.VMEM((rows, max(*share, 1) * HEAD), jnp.bfloat16),
            pltpu.VMEM((every, WINDOW, 2, rows, HEAD), jnp.bfloat16),
            pltpu.VMEM((rows, WINDOW * rows), jnp.float32),
            dma((4,)),
            pltpu.SemaphoreType.REGULAR,
            dma((every,)),
            dma((every,)),
            dma((every, PIECES)),
            dma((every, 2, 2)),
            dma((2,)),
            dma((2,)),
            dma((hops,)),
            dma((hops, heads // 2)),
            dma((hops + 2,)),
            dma((hops + 2,)),
        ],
        compiler_params=pltpu.CompilerParams(
            collective_id=0, has_side_effects=True, vmem_limit_bytes=32 * 1024 * 1024),
    )(*(pltpu.with_memory_space_constraint(z, pltpu.HBM)
        for z in (queries, keys, values, block_pos)))


def solution(mesh):
    n, T = mesh.shape["seq"], mesh.shape["tensor"]
    placed = (P("seq", "tensor"), P("seq", "tensor"), P("seq", "tensor"), P())
    return jax.shard_map(functools.partial(body, n, T), mesh=mesh, in_specs=placed,
                         out_specs=P("seq", None), check_vma=False)
```

time: 42.4 us -> 35 us (0.83)
  Pallas kernels: 40.2 us -> 32.9 us
    pallas_call x1, Pallas kernels: 40.2 us -> 32.9 us  [body(): pl.pallas_call(functools.partial(kernel, n, T, rows, groups, share), out_...]
where the time goes in v2:
time: 35 us; the launch traced here: 34.9 us
  Pallas kernels  32.9 us (94%)
  local copies, waits for them, and re-layouts  2.02 us (6%)
    pallas_call x1, Pallas kernels, body(): pl.pallas_call(functools.partial(kernel, n, T, rows, groups, share), out_...  32.9 us
    unnamed x1, local copies, waits for them, and re-layouts  2.02 us

profile of v2, /device:TPU:0, one launch (start us, length us, event | category | flops | bytes accessed | tf_op | source)
XLA Modules:
  0.0 34.9 jit_solution(11247375403801123808)
XLA Ops:
  0.0 32.9 %shard_map.46 = bf16[256,8192]{1,0:T(8,128)(2,1)S(1)} custom-call(bf16[256,2048]{1,0:T(8,128)(2,1)} %q_hbm.1, bf16[256,256]{1,0:T(8,128)(2,1)} %k_hbm.1, bf16[256,256]{1,0:T(8,128)(2,1)} %v_hbm.1, s32[16]{0:T(128)} %bp_hbm.1), custom_call_target="tpu_custom_call" | custom-call | tf_op jit(solution)/shard_map/pallas_call | solution.py:391
  32.9 2.0 %copy.6 = bf16[256,8192]{1,0:T(8,128)(2,1)} copy(bf16[256,8192]{1,0:T(8,128)(2,1)S(1)} %shard_map.46) | data formatting | bytes 8388608

commit v3 on v2

--- a/solution.py
+++ b/solution.py
@@ -15,8 +15,6 @@
 WINDOW = 4
 SHARE = (8, 0)
 AHEAD = (6, 10)
-CROSS = ((0, 1, 2, 3), (0, 1), (0, 1))
-BESIDE = ((0, 1, 2, 3), (0, 1, 2, 3), (0, 1, 2, 3))
 MESH = pl.DeviceIdType.MESH
 
 
@@ -34,12 +32,6 @@
     half = rows // 2
     cut = rows // CUTS
 
-    def cross(g):
-        return CROSS[min(g, 2)]
-
-    def beside(g):
-        return BESIDE[min(g, 2)]
-
     def seq_dev(d):
         return (lax.rem(s + d + n, n), t)
 
@@ -103,7 +95,7 @@
         return pltpu.make_async_remote_copy(
             src_ref=kv.at[g, src, i // CUTS, part], dst_ref=kv.at[g, b, i // CUTS, part],
             send_sem=(own_send if own else relay_send).at[g],
-            recv_sem=two_recv.at[g, i] if b == 2 else kind_recv.at[g, b // 2, i // CUTS],
+            recv_sem=two_recv.at[g, i] if b == 2 else kind_recv.at[g, i // CUTS],
             device_id=seq_dev(d), device_id_type=MESH)
 
     def slots(g, ref, sem):
@@ -111,8 +103,8 @@
             src_ref=ref, dst_ref=ref, send_sem=sem, recv_sem=sem,
             device_id=sibling, device_id_type=MESH)
 
-    def got(g, b, kind):
-        slots(g, kv.at[g, b, kind], kind_recv.at[g, b // 2, kind]).wait_recv()
+    def got(g, kind):
+        slots(g, kv.at[g, 0:2, kind], kind_recv.at[g, kind]).wait_recv()
 
     def send_own(g):
         for i in range(PIECES):
@@ -129,25 +121,11 @@
             @pl.when(odd == 1)
             def _():
                 kv_copy(g, i, 1, 2, -1).start()
-                if i in cross(g):
-                    kv_copy(g, i, 3, 2, 1).start()
-
-            if i in beside(g):
-                @pl.when(odd == 0)
-                def _():
-                    kv_copy(g, i, 3, 2, 1).start()
-
-    def relay_one(g, kind):
-        got(g, 1, kind)
-        for i in range(kind * CUTS, (kind + 1) * CUTS):
-            if i not in beside(g):
-                @pl.when(odd == 1)
-                def _():
-                    kv_copy(g, i, 3, 1, 2).start()
-            if i not in cross(g):
-                @pl.when(odd == 0)
-                def _():
-                    kv_copy(g, i, 3, 1, 2).start()
+                kv_copy(g, i, 3, 2, 1).start()
+
+            @pl.when(odd == 0)
+            def _():
+                kv_copy(g, i, 3, 2, 1).start()
 
     def own_sent(g):
         for parity, count in ((0, 2), (1, 1)):
@@ -156,11 +134,10 @@
                 slots(g, kv.at[g, 0:count], own_send.at[g]).wait_send()
 
     def relays_sent(g):
-        ways = len(beside(g)) - len(cross(g))
-        for parity, count in ((0, PIECES + ways), (1, 2 * PIECES - ways)):
+        for parity, count in ((0, 1), (1, 2)):
             @pl.when(odd == parity)
             def _():
-                slots(g, kv.at[g, 0:count // 2, 0], relay_send.at[g]).wait_send()
+                slots(g, kv.at[g, 0:count], relay_send.at[g]).wait_send()
 
     def keys_lent():
         return pltpu.make_async_remote_copy(
@@ -300,31 +277,22 @@
         elif g < every:
             borrowers(lambda m, first: f(g))
 
-    def first_relays(g):
-        relay_one(g, 0)
-        relay_one(g, 1)
-
     def arrive(g):
-        got(g, 3, 0)
-        got(g, 3, 1)
-
-    def late():
-        relay_one(0, 1)
-        got(0, 3, 1)
+        got(g, 0)
+        got(g, 1)
 
     for g in range(groups):
         base = g * GROUP
         if g == 0:
-            relay_one(0, 0)
-            got(0, 3, 0)
-            own_heads(0, 0, 2, late)
+            got(0, 0)
+            own_heads(0, 0, 2, lambda: got(0, 1))
             own_heads(0, 2, 2)
+            relay(1, relay_two)
         else:
+            relay(g + 1, relay_two)
             arrive(g)
             own_heads(g, base, 4)
-        relay(g + 1, relay_two)
         own_heads(g, base + 4, 4)
-        relay(g + 1, first_relays)
 
     def forwards(first, end):
         lax.fori_loop(first // 2, end // 2, forward, 0)
@@ -404,7 +372,7 @@
             dma((every,)),
             dma((every,)),
             dma((every, PIECES)),
-            dma((every, 2, 2)),
+            dma((every, 2)),
             dma((2,)),
             dma((2,)),
             dma((hops,)),

time: 35 us -> 35 us (level)
  no operation moved by 1% of the time
where the time goes in v3:
time: 35 us; the launch traced here: 34.8 us
  Pallas kernels  32.8 us (94%)
  local copies, waits for them, and re-layouts  2.02 us (6%)
    pallas_call x1, Pallas kernels, body(): pl.pallas_call(functools.partial(kernel, n, T, rows, groups, share), out_...  32.8 us
    unnamed x1, local copies, waits for them, and re-layouts  2.02 us

profile of v3, /device:TPU:0, one launch (start us, length us, event | category | flops | bytes accessed | tf_op | source)
XLA Modules:
  0.0 34.8 jit_solution(17117606795311799324)
XLA Ops:
  0.0 32.8 %shard_map.46 = bf16[256,8192]{1,0:T(8,128)(2,1)S(1)} custom-call(bf16[256,2048]{1,0:T(8,128)(2,1)} %q_hbm.1, bf16[256,256]{1,0:T(8,128)(2,1)} %k_hbm.1, bf16[256,256]{1,0:T(8,128)(2,1)} %v_hbm.1, s32[16]{0:T(128)} %bp_hbm.1), custom_call_target="tpu_custom_call" | custom-call | tf_op jit(solution)/shard_map/pallas_call | solution.py:359
  32.8 2.0 %copy.6 = bf16[256,8192]{1,0:T(8,128)(2,1)} copy(bf16[256,8192]{1,0:T(8,128)(2,1)S(1)} %shard_map.46) | data formatting | bytes 8388608
